TPU v7x, 128 devices: a whole 4x4x4 slice. The times are simulated.
128 devices in a mesh: dp: 16 (over x, y), mp: 8 (over z, core).
Axes of the slice: x: 4, y: 4, z: 4, core: 2. Of those that a mesh axis runs over, the one named last changes fastest.
Arguments:
- patches: bfloat16 [768, 64, 1024], P(('dp', 'mp')), may hold values from -6 to 6
- gain_first: float32 [1024], replicated, may hold values from 0.1 to 1.9
- joint_weight: bfloat16 [1024, 3, 1024], P('dp', None, 'mp'), may hold values from -0.1875 to 0.1875
- head_scale: float32 [16], P('mp'), may hold values from 2 to 32
- output_weight: bfloat16 [1024, 1024], P('mp', 'dp'), may hold values from -0.1875 to 0.1875
- gain_second: float32 [1024], replicated, may hold values from 0.3 to 3
- up_weight: bfloat16 [1024, 4096], P('dp', 'mp'), may hold values from -0.1875 to 0.1875
- down_weight: bfloat16 [4096, 1024], P('mp', 'dp'), may hold values from -0.09375 to 0.09375
- gain_final: float32 [1024], replicated, may hold values from 0.1 to 1.9
- project_weight: bfloat16 [1024, 768], replicated, may hold values from -0.1875 to 0.1875
- text_bank: bfloat16 [12288, 768], P(('dp', 'mp')), may hold values from -20000 to 20000
- captions: int32 [768], replicated, may hold values from 0 to 12287
- reference_loss: float32 [768], P(('dp', 'mp')), may hold values from 2 to 20
Outputs:
- learnability: float32 [768], P(('dp', 'mp'))
All inputs are finite; a program needn't handle non-finite values.
Results may differ from a plain program's by a relative error of at most 0.018.
Values may be sent and summed in bfloat16 or wider, within the bound.
No kernel may reach another device: no remote copies, remote signals or barrier semaphores. Data moves between devices by JAX's collectives and lax.ppermute only.
A program may use at most 128 MiB of HBM per device.

v0:
```python
import jax
import jax.numpy as jnp
from jax import lax
from jax.sharding import PartitionSpec as P


def gather_turned(arrays, axis, dims):
    turned = [jnp.moveaxis(a, dim, 0) for a, dim in zip(arrays, dims)]
    both = jnp.concatenate([t.reshape(len(t), -1) for t in turned], axis=1)
    result, at, outs = (lax.all_gather(both, axis, axis=0, tiled=True), 0, [])
    for t, dim in zip(turned, dims):
        slab = result[:, at : at + t[0].size].reshape(-1, *t.shape[1:])
        outs.append(jnp.moveaxis(slab, 0, dim))
        at += t[0].size
    return tuple(outs)


def joined_along(parts, dim):
    lengths = list(parts.shape[1:])
    lengths[dim] *= parts.shape[0]
    return jnp.moveaxis(parts, 0, dim).reshape(lengths)


def sent_to_all(array, axis):
    devices = lax.axis_size(axis)
    return lax.all_to_all(
        jnp.broadcast_to(array[None], (devices, *array.shape)), axis, 0, 0, tiled=True
    )


def gathered_copies(array, axis, dim):
    return joined_along(sent_to_all(array, axis), dim)


def layer_norm(values, gain):
    centre = values - jnp.mean(values, axis=-1, keepdims=True)
    spread = jnp.mean(centre * centre, axis=-1, keepdims=True)
    return centre * lax.rsqrt(spread + 1e-06) * gain


def unit_rows(values):
    return values * lax.rsqrt(jnp.sum(values * values, axis=-1, keepdims=True) + 1e-06)


def attend(normed_rows, joint_full, scales, image_count, patch_count):
    features = normed_rows.shape[1]
    local_heads = scales.shape[0]
    head_width = joint_full.shape[2] // local_heads
    joint = jnp.dot(
        normed_rows, joint_full.reshape(features, -1), preferred_element_type=jnp.float32
    )
    joint = joint.reshape(image_count, patch_count, 3, local_heads, head_width)
    queries = unit_rows(joint[:, :, 0]).astype(jnp.bfloat16)
    key_rows = unit_rows(joint[:, :, 1]).astype(jnp.bfloat16)
    value_rows = joint[:, :, 2].astype(jnp.bfloat16)
    scores = jnp.einsum("bqhd,bkhd->bhqk", queries, key_rows, preferred_element_type=jnp.float32)
    exponent = jnp.exp(scores * scales[None, :, None, None])
    attention = (exponent / jnp.sum(exponent, axis=-1, keepdims=True)).astype(jnp.bfloat16)
    head_out = jnp.einsum(
        "bhqk,bkhd->bqhd", attention, value_rows, preferred_element_type=jnp.float32
    ).astype(jnp.bfloat16)
    return head_out.reshape(image_count * patch_count, local_heads * head_width)


def grouped_local(left_rows, right_cols, groups):
    rows = left_rows.shape[0]
    group_width = left_rows.shape[1] // groups
    left_groups = left_rows.reshape(rows, groups, group_width)
    right_groups = right_cols.reshape(groups, group_width, right_cols.shape[1])
    partial_value = jnp.einsum(
        "rgk,gkn->rgn", left_groups, right_groups, preferred_element_type=jnp.float32
    )
    rounded = lax.optimization_barrier(partial_value.astype(jnp.bfloat16))
    return jnp.sum(rounded.astype(jnp.float32), axis=1)


def shards(
    patches,
    gain_first,
    joint_weight,
    head_scale,
    output_weight,
    gain_second,
    up_weight,
    down_weight,
    gain_final,
    project_weight,
    text_bank,
    captions,
    reference_loss,
):
    joint_full, output_full, up_full, down_full = gather_turned(
        (joint_weight, output_weight, up_weight, down_weight), "dp", (0, 1, 0, 1)
    )
    own_images, patch_count, features = patches.shape
    residual = patches.astype(jnp.float32)
    normed_first = layer_norm(residual, gain_first).astype(jnp.bfloat16)
    groups = lax.axis_size("mp")
    joint_all, output_all, up_all, down_all = (
        lax.all_gather(joint_full, "mp", axis=2, tiled=True),
        lax.all_gather(output_full, "mp", axis=0, tiled=True),
        lax.all_gather(up_full, "mp", axis=1, tiled=True),
        lax.all_gather(down_full, "mp", axis=0, tiled=True),
    )
    scales_all = gathered_copies(head_scale, "mp", 0)
    flat_rows = normed_first.reshape(own_images * patch_count, features)
    head_out = attend(flat_rows, joint_all, scales_all, own_images, patch_count)
    residual_flat = residual.reshape(own_images * patch_count, features)
    residual_two = residual_flat + grouped_local(head_out, output_all, groups)
    normed_second = layer_norm(residual_two, gain_second).astype(jnp.bfloat16)
    upper = jnp.dot(normed_second, up_all, preferred_element_type=jnp.float32)
    hidden = jax.nn.gelu(upper, approximate=False).astype(jnp.bfloat16)
    feed = grouped_local(hidden, down_all, groups)
    pooled = (
        jnp.sum((residual_two + feed).reshape(own_images, patch_count, features), axis=1)
        / patch_count
    )
    pooled_norm = layer_norm(pooled, gain_final).astype(jnp.bfloat16)
    embedded = jnp.dot(pooled_norm, project_weight, preferred_element_type=jnp.float32)
    image_units = unit_rows(embedded).astype(jnp.bfloat16)
    first_row = lax.axis_index(("dp", "mp")) * own_images
    own_captions = lax.dynamic_slice_in_dim(captions, first_row, own_images)
    highest = jnp.full((own_images,), -1e30, jnp.float32)
    logits = lax.dot_general(
        image_units,
        lax.all_gather(text_bank, ("dp", "mp"), axis=0, tiled=True),
        (((1,), (1,)), ((), ())),
        preferred_element_type=jnp.float32,
    )
    new_highest = jnp.maximum(highest, jnp.max(logits, axis=1))
    totals = jnp.sum(jnp.exp(logits - new_highest[:, None]), axis=1)
    text_ids = lax.broadcasted_iota(jnp.int32, logits.shape, 1)
    matched = jnp.sum(jnp.where(text_ids == own_captions[:, None], logits, 0.0), axis=1)
    highest, totals, matched = (new_highest, totals, matched)
    return highest + jnp.log(totals) - matched - reference_loss


def solution(mesh):
    placed = (
        P(("dp", "mp"), None, None),
        P(),
        P("dp", None, "mp"),
        P("mp"),
        P("mp", "dp"),
        P(),
        P("dp", "mp"),
        P("mp", "dp"),
        P(),
        P(),
        P(("dp", "mp"), None),
        P(),
        P(("dp", "mp")),
    )
    return jax.shard_map(
        shards, mesh=mesh, in_specs=placed, out_specs=P(("dp", "mp")), check_vma=False
    )
```

profile of v0, /device:TPU:1, one launch (start us, length us, event | category | flops | bytes accessed | tf_op | source)
XLA Modules:
  0.0 336.5 jit_solution(14013959427415211761)
XLA Ops:
  6.5 0.9 copy_bitcast_fusion
  7.5 1.6 pad_maximum_fusion
  9.1 50.7 %all-gather.7.cloned.1.call-done = bf16[1024,1536]{1,0:T(8,128)(2,1)} async-done(((bf16[64,1536]{1,0:T(8,128)(2,1)}), bf16[1024,1536]{1,0:T(8,128)(2,1)}) %all-gather.7.cloned.1.call-update) | async-done | bytes 3145744 | tf_op jit(solution)/shard_map/all_gather | solution.py:10
  59.8 1.2 slice.30
  61.0 1.2 copy.85
  62.3 1.0 slice.29
  63.2 0.9 copy.84
  64.2 2.7 fusion.42
  66.9 1.3 copy.86
  68.3 0.5 all-gather.17.cloned.1.call-update
  68.9 0.6 broadcast_in_dim.5
  69.5 5.7 %all-to-all-start = ((f32[8,1,2]{2,1,0:T(1,128)}), f32[8,1,2]{2,1,0:T(1,128)S(1)}, u32[]{:S(2)}, u32[]{:S(2)}) async-start(f32[8,1,2]{2,1,0:T(1,128)} %broadcast_in_dim.5), calls=%async_computation | async-start | bytes 8192 | tf_op jit(solution)/shard_map/all_to_all | solution.py:26
  75.2 1.4 copy.74
  76.6 0.2 convert_reduce_fusion.2
  76.8 0.3 multiply_reduce_fusion.3
  77.1 0.8 dynamic_slice.3
  77.9 2.1 all-to-all-done
  80.0 0.5 broadcast.129
  80.5 0.7 reduce.5
  81.2 0.1 mul.133
  81.3 22.1 %all-gather.11.cloned.1.call-done = bf16[1024,3,1024]{0,2,1:T(8,128)(2,1)} async-done(((bf16[1024,3,128]{0,2,1:T(8,128)(2,1)}), bf16[1024,3,1024]{0,2,1:T(8,128)(2,1)}) %all-gather.11.cloned.1.call-update) | async-done | bytes 6291472 | tf_op jit(solution)/shard_map/all_gather | solution.py:100
  103.3 8.1 %fusion.23 = f32[6,64,3,16,64]{1,4,3,2,0:T(8,128)S(1)} fusion(bf16[3,16,64,1024,1]{3,2,1,0,4:T(8,128)(2,1)} %bitcast.81, bf16[6,64,1024]{2,1,0:T(8,128)(2,1)S(1)} %copy-done.1, f32[1024]{0:T(1024)S(1)} %copy-done.5, f32[6,64]{1,0:T(8,128)S(1)} %add_rsqrt_fusion.3, f32[6,64]{1,0:T(8,128)S(1)} %broadcast_multiply_fusion.1), kind=kOutput, calls=%fused_computation.50 | convolution fusion | flops 2417885184 | bytes 11803648 | tf_op jit(solution)/shard_map/dot_general | solution.py:49
  111.4 1.2 multiply_reduce_fusion.1
  112.7 1.2 fusion.12
  113.9 2.0 fusion.19
  115.9 3.2 copy.69
  119.0 2.6 reshape_reshape.3
  121.7 8.8 %all-gather.9.cloned.1.call-done = bf16[1024,1024]{1,0:T(8,128)(2,1)} async-done(((bf16[128,1024]{1,0:T(8,128)(2,1)}), bf16[1024,1024]{1,0:T(8,128)(2,1)}) %all-gather.9.cloned.1.call-update) | async-done | bytes 2097168 | tf_op jit(solution)/shard_map/all_gather | solution.py:101
  130.5 3.5 %convert_bitcast_fusion.1 = bf16[384,8,1024]{0,2,1:T(8,128)(2,1)S(1)} fusion(bf16[8,128,1024]{2,1,0:T(8,128)(2,1)} %bitcast.76, bf16[384,8,128]{2,1,0:T(8,128)(2,1)S(1)} %reshape_reshape.3), kind=kOutput, calls=%fused_computation.20 | convolution fusion | flops 808452096 | bytes 9175040 | tf_op jit(solution)/shard_map/rgk,gkn->rgn/dot_general | solution.py:70
  134.0 2.0 convert_reduce_fusion.1
  136.0 3.0 copy.72
  139.0 1.6 fusion.33
  140.6 0.1 div.39
  140.7 1.9 multiply_reduce_fusion.2
  142.7 39.5 %all-gather.15.cloned.1.call-done = bf16[1024,4096]{1,0:T(8,128)(2,1)} async-done(((bf16[1024,512]{1,0:T(8,128)(2,1)}), bf16[1024,4096]{1,0:T(8,128)(2,1)}) %all-gather.15.cloned.1.call-update) | async-done | bytes 8388624 | tf_op jit(solution)/shard_map/all_gather | solution.py:102
  182.2 21.2 %fusion.2 = bf16[384,4096]{1,0:T(8,128)(2,1)} fusion(bf16[1024,4096]{1,0:T(8,128)(2,1)} %all-gather.15.cloned.1.call-done, f32[384,1024]{0,1:T(8,128)} %copy.74, f32[384,1024]{0,1:T(8,128)} %convert_reduce_fusion.1, f32[1024]{0:T(1024)S(1)} %copy-done.6, f32[384]{0:T(512)S(1)} %rsqrt.55, f32[384]{0:T(512)S(1)} %div.39), kind=kOutput, calls=%fused_computation.5 | convolution fusion | flops 3325427712 | bytes 14687232 | tf_op jit(solution)/shard_map/dot_general | solution.py:111
  203.4 30.3 %all-gather.13.cloned.1.call-done = bf16[4096,1024]{1,0:T(8,128)(2,1)} async-done(((bf16[512,1024]{1,0:T(8,128)(2,1)}), bf16[4096,1024]{1,0:T(8,128)(2,1)}) %all-gather.13.cloned.1.call-update) | async-done | bytes 8388624 | tf_op jit(solution)/shard_map/all_gather | solution.py:103
  233.7 11.9 %convert_bitcast_fusion = bf16[384,8,1024]{0,2,1:T(8,128)(2,1)} fusion(bf16[8,512,1024]{2,1,0:T(8,128)(2,1)} %bitcast.80, bf16[48,8,8,512]{3,2,1,0:T(8,128)(2,1)} %bitcast.82), kind=kOutput, calls=%fused_computation.6 | convolution fusion | flops 3224371200 | bytes 17825792 | tf_op jit(solution)/shard_map/rgk,gkn->rgn/dot_general | solution.py:70
  245.6 5.1 %convert_reduce_fusion = f32[384,1024]{0,1:T(8,128)} fusion(bf16[384,8,1024]{0,2,1:T(8,128)(2,1)} %convert_bitcast_fusion), kind=kLoop, calls=%fused_computation | loop fusion | flops 5898240 | bytes 7864320 | tf_op jit(solution)/shard_map/reduce_sum | solution.py:74
  250.6 3.0 copy.77
  253.7 2.3 add_reduce_fusion
  256.0 0.1 multiply_reduce_fusion.5
  256.1 0.2 multiply_reduce_fusion.4
  256.3 0.5 multiply_reduce_fusion.6
  256.8 62.9 %all-gather.17.cloned.1.call-done = bf16[12288,768]{1,0:T(8,128)(2,1)} async-done(((bf16[96,768]{1,0:T(8,128)(2,1)}), bf16[12288,768]{1,0:T(8,128)(2,1)}) %all-gather.17.cloned.1.call-update) | async-done | bytes 18874384 | tf_op jit(solution)/shard_map/all_gather | solution.py:126
  319.7 9.0 %fusion.43 = (f32[6]{0:T(128)S(1)}, f32[6,12288]{1,0:T(8,128)S(1)}) fusion(bf16[12288,768]{1,0:T(8,128)(2,1)} %all-gather.17.cloned.1.call-done, f32[6,768]{1,0:T(8,128)S(1)} %get-tuple-element.14, f32[6]{0:T(128)S(1)} %add_rsqrt_fusion.4), kind=kOutput, calls=%fused_computation.90 | convolution fusion | flops 113329144 | bytes 19187760 | tf_op jit(solution)/shard_map/dot_general | solution.py:124
  328.8 0.3 exponential_reduce_fusion
  329.1 0.5 subtract_subtract_fusion
  (35 shorter events, 0.5 us)
Async XLA Ops:
  6.5 249.8 %copy-start = (bf16[1024,768]{1,0:T(8,128)(2,1)S(1)}, bf16[1024,768]{1,0:T(8,128)(2,1)}, u32[]{:S(2)}) copy-start(bf16[1024,768]{1,0:T(8,128)(2,1)} %param.22) | copy-start | bytes 4718596
  6.5 53.2 %all-gather.7.cloned.1.call-start = ((), (), s32[]{:S(2)}) async-start(), calls=%async_computation.1 | async-start | bytes 3342336 | tf_op jit(solution)/shard_map/all_gather | solution.py:10
  9.1 94.3 %all-gather.11.cloned.1.call-start = ((), (), s32[]{:S(2)}) async-start(), calls=%async_computation.3 | async-start | bytes 7077888 | tf_op jit(solution)/shard_map/all_gather | solution.py:100
  61.0 7.9 %copy-start.3 = (f32[2]{0:T(128)S(1)}, f32[2]{0:T(128)}, u32[]{:S(2)}) copy-start(f32[2]{0:T(128)} %param.16) | copy-start | bytes 28
  61.0 14.2 %copy-start.1 = (bf16[6,64,1024]{2,1,0:T(8,128)(2,1)S(1)}, bf16[6,64,1024]{2,1,0:T(8,128)(2,1)}, u32[]{:S(2)}) copy-start(bf16[6,64,1024]{2,1,0:T(8,128)(2,1)} %param.13) | copy-start | bytes 2359300
  62.2 68.3 %all-gather.9.cloned.1.call-start = ((), (), s32[]{:S(2)}) async-start(), calls=%async_computation.2 | async-start | bytes 2359296 | tf_op jit(solution)/shard_map/all_gather | solution.py:101
  64.1 39.2 %copy-start.5 = (f32[1024]{0:T(1024)S(1)}, f32[1024]{0:T(1024)}, u32[]{:S(2)}) copy-start(f32[1024]{0:T(1024)} %param.14) | copy-start | bytes 12292
  64.1 118.1 %all-gather.15.cloned.1.call-start = ((), (), s32[]{:S(2)}) async-start(), calls=%async_computation.5 | async-start | bytes 9437184 | tf_op jit(solution)/shard_map/all_gather | solution.py:102
  66.9 166.8 %all-gather.13.cloned.1.call-start = ((), (), s32[]{:S(2)}) async-start(), calls=%async_computation.4 | async-start | bytes 9437184 | tf_op jit(solution)/shard_map/all_gather | solution.py:103
  68.3 251.4 %all-gather.17.cloned.1.call-start = ((), (), s32[]{:S(2)}) async-start(), calls=%async_computation.6 | async-start | bytes 19021824 | tf_op jit(solution)/shard_map/all_gather | solution.py:126
  69.5 10.5 %all-to-all-start = ((f32[8,1,2]{2,1,0:T(1,128)}), f32[8,1,2]{2,1,0:T(1,128)S(1)}, u32[]{:S(2)}, u32[]{:S(2)}) async-start(f32[8,1,2]{2,1,0:T(1,128)} %broadcast_in_dim.5), calls=%async_computation | async-start | bytes 8192 | tf_op jit(solution)/shard_map/all_to_all | solution.py:26
  134.0 48.2 %copy-start.6 = (f32[1024]{0:T(1024)S(1)}, f32[1024]{0:T(1024)}, u32[]{:S(2)}) copy-start(f32[1024]{0:T(1024)} %param.18) | copy-start | bytes 12292
  245.6 10.8 %copy-start.2 = (f32[1024]{0:T(1024)S(1)}, f32[1024]{0:T(1024)}, u32[]{:S(2)}) copy-start(f32[1024]{0:T(1024)} %param.21) | copy-start | bytes 12292
  319.7 9.4 %copy-start.4 = (f32[6]{0:T(128)S(1)}, f32[6]{0:T(128)}, u32[]{:S(2)}) copy-start(f32[6]{0:T(128)} %param.25) | copy-start | bytes 76
Sparse Core Ops, SparseCore 0:
  9.5 50.2 all-gather.6
  62.3 40.9 all-gather.10
  105.0 25.4 all-gather.8
  132.0 50.1 all-gather.14
  183.8 49.8 all-gather.12
  236.6 83.0 all-gather.16
where the time goes:
time: 337 us; the launch traced here: 336 us
  waiting for transfers between devices  217 us (64%)
  matrix products  57.3 us (17%)
  local copies, waits for them, and re-layouts  24.5 us (7%)
  other arithmetic  18.1 us (5%)
  between operations  13.7 us (4%)
  starting transfers between devices  5.93 us (2%)
    all_gather x1, waiting for transfers between devices, shards(): lax.all_gather(text_bank, ('dp', 'mp'), axis=0, tiled=True)  62.9 us
    all_gather x1, waiting for transfers between devices, gather_turned(): result, at, outs = (lax.all_gather(both, axis, axis=0, tiled=True), 0, [])  50.7 us
    all_gather x1, waiting for transfers between devices, shards(): lax.all_gather(up_full, 'mp', axis=1, tiled=True)  39.5 us
    all_gather x1, waiting for transfers between devices, shards(): lax.all_gather(down_full, 'mp', axis=0, tiled=True)  30.3 us
    all_gather x1, waiting for transfers between devices, shards(): lax.all_gather(joint_full, 'mp', axis=2, tiled=True)  22.1 us
    dot_general x1, matrix products, shards(): upper = jnp.dot(normed_second, up_all, preferred_element_type=jnp.float32)  21.2 us
    dot_general x2, matrix products, grouped_local(): jnp.einsum('rgk,gkn->rgn', left_groups, right_groups, preferred_element_t...  15.4 us
    dot_general x1, matrix products, shards(): lax.dot_general(image_units, lax.all_gather(text_bank, ('dp', 'mp'), axis...  9.03 us
  transfers between devices with their start and end apart: 7, of which 7 were waited for; matrix products, arithmetic and copies ran while one was open for 25% of the time, Pallas kernels for 0%

commit v1 on v0

--- a/solution.py
+++ b/solution.py
@@ -2,6 +2,19 @@
 import jax.numpy as jnp
 from jax import lax
 from jax.sharding import PartitionSpec as P
+
+
+def ring_gather(value, axis, dim):
+    ways = lax.axis_size(axis)
+    up = [(d, (d + 1) % ways) for d in range(ways)]
+    down = [(d, (d - 1) % ways) for d in range(ways)]
+    earlier, later = ([value], [value])
+    for _ in range(ways // 2):
+        earlier.append(lax.ppermute(earlier[-1], axis, up))
+    for _ in range((ways - 1) // 2):
+        later.append(lax.ppermute(later[-1], axis, down))
+    line = jnp.concatenate([*earlier[::-1], *later[1:]], axis=dim)
+    return jnp.roll(line, (lax.axis_index(axis) - ways // 2) * value.shape[dim], axis=dim)
 
 
 def gather_turned(arrays, axis, dims):
@@ -97,7 +110,7 @@
     normed_first = layer_norm(residual, gain_first).astype(jnp.bfloat16)
     groups = lax.axis_size("mp")
     joint_all, output_all, up_all, down_all = (
-        lax.all_gather(joint_full, "mp", axis=2, tiled=True),
+        ring_gather(joint_full, "mp", 2),
         lax.all_gather(output_full, "mp", axis=0, tiled=True),
         lax.all_gather(up_full, "mp", axis=1, tiled=True),
         lax.all_gather(down_full, "mp", axis=0, tiled=True),

time: 337 us -> 310 us (0.920)
  waiting for transfers between devices: 217 us -> 138 us
  local copies, waits for them, and re-layouts: 24.5 us -> 56.3 us
  starting transfers between devices: 5.93 us -> 27.6 us
    ppermute x0 -> x7, waiting for transfers between devices: none -> 42.1 us  [the longest x4 41.8 us: ring_gather(): earlier.append(lax.ppermute(earlier[-1], axis, up))]
    all_gather x1, waiting for transfers between devices: 39.5 us -> 0.01 us  [shards(): lax.all_gather(up_full, 'mp', axis=1, tiled=True)]
    all_gather x1, waiting for transfers between devices: 62.9 us -> 31.6 us  [shards(): lax.all_gather(text_bank, ('dp', 'mp'), axis=0, tiled=True)]
    all_gather x1, waiting for transfers between devices: 30.3 us -> 0.01 us  [shards(): lax.all_gather(down_full, 'mp', axis=0, tiled=True)]
    unnamed x17 -> x40, local copies, waits for them, and re-layouts: 3.4 us -> 29.5 us
    all_gather x1 -> x0, waiting for transfers between devices: 22.1 us -> none  [shards(): lax.all_gather(joint_full, 'mp', axis=2, tiled=True)]
    ppermute x0 -> x7, starting transfers between devices: none -> 19.1 us  [the longest x4 10 us: ring_gather(): earlier.append(lax.ppermute(earlier[-1], axis, up))]
    all_to_all x1, waiting for transfers between devices: 2.1 us -> 13.4 us  [sent_to_all(): lax.all_to_all(jnp.broadcast_to(array[None], (devices, *array.shape)), ax...]
  transfers between devices with their start and end apart: 7 -> 13, of which waited for: 7 -> 7; matrix products, arithmetic and copies ran while one was open for 25% -> 37% of each run, Pallas kernels for 0% -> 0%
where the time goes in v1:
time: 310 us; the launch traced here: 309 us
  waiting for transfers between devices  138 us (45%)
  local copies, waits for them, and re-layouts  56.3 us (18%)
  matrix products  55 us (18%)
  starting transfers between devices  27.6 us (9%)
  other arithmetic  18 us (6%)
  between operations  13.3 us (4%)
    all_gather x1, waiting for transfers between devices, gather_turned(): result, at, outs = (lax.all_gather(both, axis, axis=0, tiled=True), 0, [])  50.7 us
    ppermute x4, waiting for transfers between devices, ring_gather(): earlier.append(lax.ppermute(earlier[-1], axis, up))  41.8 us
    all_gather x1, waiting for transfers between devices, shards(): lax.all_gather(text_bank, ('dp', 'mp'), axis=0, tiled=True)  31.6 us
    unnamed x40, local copies, waits for them, and re-layouts  29.5 us
    dot_general x1, matrix products, shards(): upper = jnp.dot(normed_second, up_all, preferred_element_type=jnp.float32)  21.3 us
    dot_general x2, matrix products, grouped_local(): jnp.einsum('rgk,gkn->rgn', left_groups, right_groups, preferred_element_t...  15.5 us
    all_to_all x1, waiting for transfers between devices, sent_to_all(): lax.all_to_all(jnp.broadcast_to(array[None], (devices, *array.shape)), ax...  13.4 us
    ppermute x4, starting transfers between devices, ring_gather(): earlier.append(lax.ppermute(earlier[-1], axis, up))  10 us
  transfers between devices with their start and end apart: 13, of which 7 were waited for; matrix products, arithmetic and copies ran while one was open for 37% of the time, Pallas kernels for 0%

profile of v1, /device:TPU:1, one launch (start us, length us, event | category | flops | bytes accessed | tf_op | source)
XLA Modules:
  0.0 308.6 jit_solution(4564933260877346295)
XLA Ops:
  7.5 1.6 pad_maximum_fusion
  9.1 50.7 %all-gather.6.cloned.1.call-done = bf16[1024,1536]{1,0:T(8,128)(2,1)} async-done(((bf16[64,1536]{1,0:T(8,128)(2,1)}), bf16[1024,1536]{1,0:T(8,128)(2,1)}) %all-gather.6.cloned.1.call-update) | async-done | bytes 3145744 | tf_op jit(solution)/shard_map/all_gather | solution.py:23
  59.8 1.0 slice.29
  61.7 2.7 fusion.42
  64.4 1.3 copy.86
  66.4 2.1 slice.30
  68.5 1.4 copy.85
  69.9 2.5 collective-permute-start
  72.4 15.9 %collective-permute-done = bf16[1024,3,128]{0,2,1:T(8,128)(2,1)S(1)} collective-permute-done((bf16[1024,3,128]{0,2,1:T(8,128)(2,1)S(1)}, bf16[1024,3,128]{0,2,1:T(8,128)(2,1)S(1)}, u32[]{:S(2)}, u32[]{:S(2)}) %collective-permute-start) | collective-permute-done | bytes 786464 | tf_op jit(solution)/shard_map/ppermute | solution.py:13
  88.3 2.5 collective-permute-start.1
  90.8 1.5 collective-permute-start.4
  92.3 7.4 %collective-permute-done.1 = bf16[1024,3,128]{0,2,1:T(8,128)(2,1)S(1)} collective-permute-done((bf16[1024,3,128]{0,2,1:T(8,128)(2,1)S(1)}, bf16[1024,3,128]{0,2,1:T(8,128)(2,1)S(1)}, u32[]{:S(2)}, u32[]{:S(2)}) %collective-permute-start.1) | collective-permute-done | bytes 786464 | tf_op jit(solution)/shard_map/ppermute | solution.py:13
  99.7 2.5 collective-permute-start.2
  102.5 7.0 %collective-permute-start.5 = (bf16[1024,3,128]{0,2,1:T(8,128)(2,1)}, bf16[1024,3,128]{0,2,1:T(8,128)(2,1)}, u32[]{:S(2)}, u32[]{:S(2)}) collective-permute-start(bf16[1024,3,128]{0,2,1:T(8,128)(2,1)} %collective-permute-done.4), channel_id=1, source_target_pairs={{0,7},{1,0},{2,1},{3,2},{4,3},{5,4},{6,5},{7,6},{8,15},{9,8},{10,9... | collective-permute-start | bytes 2359304 | tf_op jit(solution)/shard_map/ppermute | solution.py:15
  109.5 18.4 %collective-permute-done.2 = bf16[1024,3,128]{0,2,1:T(8,128)(2,1)} collective-permute-done((bf16[1024,3,128]{0,2,1:T(8,128)(2,1)S(1)}, bf16[1024,3,128]{0,2,1:T(8,128)(2,1)}, u32[]{:S(2)}, u32[]{:S(2)}) %collective-permute-start.2) | collective-permute-done | bytes 786464 | tf_op jit(solution)/shard_map/ppermute | solution.py:13
  128.0 2.6 collective-permute-start.3
  131.2 8.3 %all-to-all-start = ((f32[8,1,2]{2,1,0:T(1,128)}), f32[8,1,2]{2,1,0:T(1,128)S(1)}, u32[]{:S(2)}, u32[]{:S(2)}) async-start(f32[8,1,2]{2,1,0:T(1,128)} %broadcast_in_dim.5), calls=%async_computation | async-start | bytes 8192 | tf_op jit(solution)/shard_map/all_to_all | solution.py:39
  139.5 1.4 copy.74
  142.2 13.4 %all-to-all-done = f32[8,1,2]{2,1,0:T(1,128)S(1)} async-done(((f32[8,1,2]{2,1,0:T(1,128)}), f32[8,1,2]{2,1,0:T(1,128)S(1)}, u32[]{:S(2)}, u32[]{:S(2)}) %all-to-all-start) | async-done | bytes 96 | tf_op jit(solution)/shard_map/all_to_all | solution.py:39
  157.3 2.1 constant_dynamic-update-slice_fusion.15
  159.5 2.1 constant_dynamic-update-slice_fusion.14
  161.5 2.2 constant_dynamic-update-slice_fusion.13
  163.7 2.2 constant_dynamic-update-slice_fusion.12
  166.9 2.2 constant_dynamic-update-slice_fusion.10
  169.1 2.1 constant_dynamic-update-slice_fusion.9
  172.1 2.0 constant_dynamic-update-slice_fusion.7
  174.2 2.1 constant_dynamic-update-slice_fusion.6
  179.0 2.1 constant_dynamic-update-slice_fusion.2
  181.2 2.1 constant_dynamic-update-slice_fusion.1
  184.1 3.7 %constant_dynamic-slice_fusion = bf16[1024,3,1024]{0,2,1:T(8,128)(2,1)S(1)} fusion(bf16[1024,3,2048]{0,2,1:T(8,128)(2,1)} %constant_dynamic-update-slice_fusion, s32[]{:T(128)S(6)} %select_n.21), kind=kLoop, calls=%fused_computation.104 | loop fusion | bytes 12582916 | tf_op jit(solution)/shard_map/jit(_roll_dynamic)/dynamic_slice | solution.py:17
  187.8 5.6 %fusion.23 = f32[6,64,3,16,64]{1,4,3,2,0:T(8,128)S(1)} fusion(bf16[3,16,64,1024,1]{3,2,1,0,4:T(8,128)(2,1)S(1)} %bitcast.77, bf16[6,64,1024]{2,1,0:T(8,128)(2,1)S(1)} %copy-done.1, f32[1024]{0:T(1024)S(1)} %copy-done.9, f32[6,64]{1,0:T(8,128)S(1)} %add_rsqrt_fusion.3, f32[6,64]{1,0:T(8,128)S(1)} %broadcast_multiply_fusion.1), kind=kOutput, calls=%fused_computation.50 | convolution fusion | flops 2417885184 | bytes 11803648 | tf_op jit(solution)/shard_map/dot_general | solution.py:62
  193.4 1.2 multiply_reduce_fusion.1
  194.7 1.2 fusion.12
  195.8 2.0 fusion.19
  197.9 3.2 %copy.69 = bf16[6,64,16,64]{3,2,1,0:T(8,128)(2,1)} copy(bf16[6,64,16,64]{1,3,2,0:T(8,128)(2,1)} %fusion.19) | data formatting | bytes 1572864 | tf_op jit(solution)/shard_map/convert_element_type | solution.py:74
  201.0 2.8 reshape_reshape.3
  203.8 3.6 %convert_bitcast_fusion.1 = bf16[384,8,1024]{0,2,1:T(8,128)(2,1)S(1)} fusion(bf16[8,128,1024]{2,1,0:T(8,128)(2,1)} %bitcast.80, bf16[384,8,128]{2,1,0:T(8,128)(2,1)S(1)} %reshape_reshape.3), kind=kOutput, calls=%fused_computation.20 | convolution fusion | flops 808452096 | bytes 9175040 | tf_op jit(solution)/shard_map/rgk,gkn->rgn/dot_general | solution.py:83
  207.4 2.0 convert_reduce_fusion.1
  209.5 3.0 copy.72
  212.5 1.6 fusion.33
  214.2 1.8 multiply_reduce_fusion.2
  216.1 21.3 %fusion.2 = bf16[384,4096]{1,0:T(8,128)(2,1)} fusion(bf16[1024,4096]{1,0:T(8,128)(2,1)} %all-gather.12.cloned.1.call-done, f32[384,1024]{0,1:T(8,128)} %copy.74, f32[384,1024]{0,1:T(8,128)} %convert_reduce_fusion.1, f32[1024]{0:T(1024)S(1)} %copy-done.10, f32[384]{0:T(512)S(1)} %rsqrt.55, f32[384]{0:T(512)S(1)} %div.39), kind=kOutput, calls=%fused_computation.5 | convolution fusion | flops 3325427712 | bytes 14687232 | tf_op jit(solution)/shard_map/dot_general | solution.py:124
  237.3 11.9 %convert_bitcast_fusion = bf16[384,8,1024]{0,2,1:T(8,128)(2,1)} fusion(bf16[8,512,1024]{2,1,0:T(8,128)(2,1)} %bitcast.84, bf16[48,8,8,512]{3,2,1,0:T(8,128)(2,1)} %bitcast.85), kind=kOutput, calls=%fused_computation.6 | convolution fusion | flops 3224371200 | bytes 17825792 | tf_op jit(solution)/shard_map/rgk,gkn->rgn/dot_general | solution.py:83
  249.3 5.1 %convert_reduce_fusion = f32[384,1024]{0,1:T(8,128)} fusion(bf16[384,8,1024]{0,2,1:T(8,128)(2,1)} %convert_bitcast_fusion), kind=kLoop, calls=%fused_computation | loop fusion | flops 5898240 | bytes 7864320 | tf_op jit(solution)/shard_map/reduce_sum | solution.py:87
  254.3 3.0 copy.77
  257.4 2.3 add_reduce_fusion
  260.5 31.6 %all-gather.14.cloned.1.call-done = bf16[12288,768]{1,0:T(8,128)(2,1)} async-done(((bf16[96,768]{1,0:T(8,128)(2,1)}), bf16[12288,768]{1,0:T(8,128)(2,1)}) %all-gather.14.cloned.1.call-update) | async-done | bytes 18874384 | tf_op jit(solution)/shard_map/all_gather | solution.py:139
  292.1 9.0 %fusion.43 = (f32[6]{0:T(128)S(1)}, f32[6,12288]{1,0:T(8,128)S(1)}) fusion(bf16[12288,768]{1,0:T(8,128)(2,1)} %all-gather.14.cloned.1.call-done, f32[6,768]{1,0:T(8,128)S(1)} %get-tuple-element.14, f32[6]{0:T(128)S(1)} %add_rsqrt_fusion.4), kind=kOutput, calls=%fused_computation.107 | convolution fusion | flops 113329144 | bytes 19187760 | tf_op jit(solution)/shard_map/dot_general | solution.py:137
  (71 shorter events, 14.0 us)
Async XLA Ops:
  6.5 253.5 %copy-start = (bf16[1024,768]{1,0:T(8,128)(2,1)S(1)}, bf16[1024,768]{1,0:T(8,128)(2,1)}, u32[]{:S(2)}) copy-start(bf16[1024,768]{1,0:T(8,128)(2,1)} %param.22) | copy-start | bytes 4718596
  6.5 53.2 %all-gather.6.cloned.1.call-start = ((), (), s32[]{:S(2)}) async-start(), calls=%async_computation.1 | async-start | bytes 3342336 | tf_op jit(solution)/shard_map/all_gather | solution.py:23
  9.0 194.8 %all-gather.8.cloned.1.call-start = ((), (), s32[]{:S(2)}) async-start(), calls=%async_computation.2 | async-start | bytes 2359296 | tf_op jit(solution)/shard_map/all_gather | solution.py:114
  60.7 69.8 %copy-start.7 = (f32[2]{0:T(128)S(1)}, f32[2]{0:T(128)}, u32[]{:S(2)}) copy-start(f32[2]{0:T(128)} %param.16) | copy-start | bytes 28
  60.8 78.7 %copy-start.1 = (bf16[6,64,1024]{2,1,0:T(8,128)(2,1)S(1)}, bf16[6,64,1024]{2,1,0:T(8,128)(2,1)}, u32[]{:S(2)}) copy-start(bf16[6,64,1024]{2,1,0:T(8,128)(2,1)} %param.13) | copy-start | bytes 2359300
  61.6 154.4 %all-gather.12.cloned.1.call-start = ((), (), s32[]{:S(2)}) async-start(), calls=%async_computation.4 | async-start | bytes 9437184 | tf_op jit(solution)/shard_map/all_gather | solution.py:115
  64.4 173.0 %all-gather.10.cloned.1.call-start = ((), (), s32[]{:S(2)}) async-start(), calls=%async_computation.3 | async-start | bytes 9437184 | tf_op jit(solution)/shard_map/all_gather | solution.py:116
  65.8 226.3 %all-gather.14.cloned.1.call-start = ((), (), s32[]{:S(2)}) async-start(), calls=%async_computation.5 | async-start | bytes 19021824 | tf_op jit(solution)/shard_map/all_gather | solution.py:139
  69.9 18.4 %collective-permute-start = (bf16[1024,3,128]{0,2,1:T(8,128)(2,1)S(1)}, bf16[1024,3,128]{0,2,1:T(8,128)(2,1)S(1)}, u32[]{:S(2)}, u32[]{:S(2)}) collective-permute-start(bf16[1024,3,128]{0,2,1:T(8,128)(2,1)S(1)} %bitcast.73), channel_id=1, source_target_pairs={{0,1},{1,2},{2,3},{3,4},{4,5},{5,6},{6,7},{7,0},{8,9},{9,10},{10,1... | collective-permute-start | bytes 2359304 | tf_op jit(solution)/shard_map/ppermute | solution.py:13
  88.3 14.2 %copy-start.2 = (bf16[1024,3,128]{0,2,1:T(8,128)(2,1)}, bf16[1024,3,128]{0,2,1:T(8,128)(2,1)S(1)}, u32[]{:S(2)}) copy-start(bf16[1024,3,128]{0,2,1:T(8,128)(2,1)S(1)} %collective-permute-done) | copy-start | bytes 2359300
  88.3 11.4 %collective-permute-start.1 = (bf16[1024,3,128]{0,2,1:T(8,128)(2,1)S(1)}, bf16[1024,3,128]{0,2,1:T(8,128)(2,1)S(1)}, u32[]{:S(2)}, u32[]{:S(2)}) collective-permute-start(bf16[1024,3,128]{0,2,1:T(8,128)(2,1)S(1)} %collective-permute-done), channel_id=1, source_target_pairs={{0,1},{1,2},{2,3},{3,4},{4,5},{5,6},{6,7},{7,0},{8,9},{9,10},{10,1... | collective-permute-start | bytes 2359304 | tf_op jit(solution)/shard_map/ppermute | solution.py:13
  90.8 11.7 %collective-permute-start.4 = (bf16[1024,3,128]{0,2,1:T(8,128)(2,1)S(1)}, bf16[1024,3,128]{0,2,1:T(8,128)(2,1)}, u32[]{:S(2)}, u32[]{:S(2)}) collective-permute-start(bf16[1024,3,128]{0,2,1:T(8,128)(2,1)S(1)} %bitcast.74), channel_id=1, source_target_pairs={{0,7},{1,0},{2,1},{3,2},{4,3},{5,4},{6,5},{7,6},{8,15},{9,8},{10,9... | collective-permute-start | bytes 2359304 | tf_op jit(solution)/shard_map/ppermute | solution.py:15
  99.7 9.8 %copy-start.4 = (bf16[1024,3,128]{0,2,1:T(8,128)(2,1)}, bf16[1024,3,128]{0,2,1:T(8,128)(2,1)S(1)}, u32[]{:S(2)}) copy-start(bf16[1024,3,128]{0,2,1:T(8,128)(2,1)S(1)} %collective-permute-done.1) | copy-start | bytes 2359300
  99.7 28.2 %collective-permute-start.2 = (bf16[1024,3,128]{0,2,1:T(8,128)(2,1)S(1)}, bf16[1024,3,128]{0,2,1:T(8,128)(2,1)}, u32[]{:S(2)}, u32[]{:S(2)}) collective-permute-start(bf16[1024,3,128]{0,2,1:T(8,128)(2,1)S(1)} %collective-permute-done.1), channel_id=1, source_target_pairs={{0,1},{1,2},{2,3},{3,4},{4,5},{5,6},{6,7},{7,0},{8,9},{9,10},{10,1... | collective-permute-start | bytes 2359304 | tf_op jit(solution)/shard_map/ppermute | solution.py:13
  102.5 54.3 %collective-permute-start.5 = (bf16[1024,3,128]{0,2,1:T(8,128)(2,1)}, bf16[1024,3,128]{0,2,1:T(8,128)(2,1)}, u32[]{:S(2)}, u32[]{:S(2)}) collective-permute-start(bf16[1024,3,128]{0,2,1:T(8,128)(2,1)} %collective-permute-done.4), channel_id=1, source_target_pairs={{0,7},{1,0},{2,1},{3,2},{4,3},{5,4},{6,5},{7,6},{8,15},{9,8},{10,9... | collective-permute-start | bytes 2359304 | tf_op jit(solution)/shard_map/ppermute | solution.py:15
  128.0 29.4 %collective-permute-start.3 = (bf16[1024,3,128]{0,2,1:T(8,128)(2,1)}, bf16[1024,3,128]{0,2,1:T(8,128)(2,1)}, u32[]{:S(2)}, u32[]{:S(2)}) collective-permute-start(bf16[1024,3,128]{0,2,1:T(8,128)(2,1)} %collective-permute-done.2), channel_id=1, source_target_pairs={{0,1},{1,2},{2,3},{3,4},{4,5},{5,6},{6,7},{7,0},{8,9},{9,10},{10,1... | collective-permute-start | bytes 2359304 | tf_op jit(solution)/shard_map/ppermute | solution.py:13
  131.2 24.4 %all-to-all-start = ((f32[8,1,2]{2,1,0:T(1,128)}), f32[8,1,2]{2,1,0:T(1,128)S(1)}, u32[]{:S(2)}, u32[]{:S(2)}) async-start(f32[8,1,2]{2,1,0:T(1,128)} %broadcast_in_dim.5), calls=%async_computation | async-start | bytes 8192 | tf_op jit(solution)/shard_map/all_to_all | solution.py:39
  156.8 14.4 %collective-permute-start.6 = (bf16[1024,3,128]{0,2,1:T(8,128)(2,1)}, bf16[1024,3,128]{0,2,1:T(8,128)(2,1)S(1)}, u32[]{:S(2)}, u32[]{:S(2)}) collective-permute-start(bf16[1024,3,128]{0,2,1:T(8,128)(2,1)} %collective-permute-done.5), channel_id=1, source_target_pairs={{0,7},{1,0},{2,1},{3,2},{4,3},{5,4},{6,5},{7,6},{8,15},{9,8},{10,9... | collective-permute-start | bytes 2359304 | tf_op jit(solution)/shard_map/ppermute | solution.py:15
  161.5 14.7 %copy-start.5 = (bf16[1024,3,128]{0,2,1:T(8,128)(2,1)S(1)}, bf16[1024,3,128]{0,2,1:T(8,128)(2,1)}, u32[]{:S(2)}) copy-start(bf16[1024,3,128]{0,2,1:T(8,128)(2,1)} %copy-done.4) | copy-start | bytes 2359300
  163.7 13.5 %copy-start.3 = (bf16[1024,3,128]{0,2,1:T(8,128)(2,1)S(1)}, bf16[1024,3,128]{0,2,1:T(8,128)(2,1)}, u32[]{:S(2)}) copy-start(bf16[1024,3,128]{0,2,1:T(8,128)(2,1)} %copy-done.2) | copy-start | bytes 2359300
  184.1 3.7 %copy-start.9 = (f32[1024]{0:T(1024)S(1)}, f32[1024]{0:T(1024)}, u32[]{:S(2)}) copy-start(f32[1024]{0:T(1024)} %param.14) | copy-start | bytes 12292
  207.4 8.6 %copy-start.10 = (f32[1024]{0:T(1024)S(1)}, f32[1024]{0:T(1024)}, u32[]{:S(2)}) copy-start(f32[1024]{0:T(1024)} %param.18) | copy-start | bytes 12292
  249.3 10.8 %copy-start.6 = (f32[1024]{0:T(1024)S(1)}, f32[1024]{0:T(1024)}, u32[]{:S(2)}) copy-start(f32[1024]{0:T(1024)} %param.21) | copy-start | bytes 12292
  292.1 9.4 %copy-start.8 = (f32[6]{0:T(128)S(1)}, f32[6]{0:T(128)}, u32[]{:S(2)}) copy-start(f32[6]{0:T(128)} %param.25) | copy-start | bytes 76
Sparse Core Ops, SparseCore 0:
  9.5 50.2 all-gather.5
  61.8 27.6 all-gather.7
  91.2 62.0 all-gather.11
  154.8 51.2 all-gather.9
  209.0 83.0 all-gather.13
